TPU v7x, 32 devices: a whole 2x2x4 slice. The times are simulated.
32 devices in a mesh: leaf: 2 (over core), row: 4 (over y, x), col: 4 (over z).
Axes of the slice: x: 2, y: 2, z: 4, core: 2. Of those that a mesh axis runs over, the one named last changes fastest.
Arguments:
- rhs_leaf: bfloat16 [2, 8, 64, 2048], P('leaf', None, None, 'col'), may hold values from -6 to 6
- dinv_leaf: bfloat16 [2, 8, 2048, 2048], P('leaf', None, 'row', 'col'), as said below
- panel_leaf: bfloat16 [2, 8, 1024, 2048], P('leaf', None, 'col', 'row'), may hold values from -0.0625 to 0.0625
- counts: int32 [2, 8], P('leaf'), may hold values from 256 to 2048, as said below
- row_index: int32 [2, 8, 1024], P('leaf'), may hold values from 0 to 4095, as said below
- rhs_root: bfloat16 [64, 4096], P(None, 'col'), may hold values from -6 to 6
- dinv_root: bfloat16 [4096, 4096], P(('leaf', 'row')), as said below
Outputs:
- y_leaf: bfloat16 [2, 8, 64, 2048], P('leaf', None, None, 'row')
- y_root: bfloat16 [64, 4096], P(None, ('leaf', 'row'))
Inputs may be any that keep to these rules, and one draw needn't show every extreme that they name: `counts`: each subtree supernode has at least 256 columns; at least one supernode of every draw has all 2048. `row_index`: within one supernode the 1024 entries are distinct and increasing. `dinv_leaf`: each [2048, 2048] block is lower triangular with a nonzero diagonal. `dinv_root`: lower triangular with a nonzero diagonal.
All inputs are finite; a program needn't handle non-finite values.
Results may differ from a plain program's by a relative error of at most 0.0053.
Values may be sent and summed in bfloat16 or wider, within the bound.
No kernel may reach another device: no remote copies, remote signals or barrier semaphores. Data moves between devices by JAX's collectives and lax.ppermute only.
A program may use at most 64 MiB of HBM per device.

v0:
```python
import jax
import jax.numpy as jnp
from jax import lax
from jax.sharding import PartitionSpec as P


def local(rhs_leaf, dinv_leaf, panel_leaf, counts, row_index, rhs_root, dinv_root):
    width_col = rhs_leaf.shape[3]
    width_row = dinv_leaf.shape[2]
    panel_rows = panel_leaf.shape[2]
    columns = rhs_root.shape[0]
    sep_width = rhs_root.shape[1] * lax.axis_size("col")
    limit = counts[0][:, None, None]
    col_slots = lax.axis_index("col") * width_col + lax.iota(jnp.int32, width_col)
    masked = jnp.where(col_slots[None, None, :] < limit, rhs_leaf[0], jnp.zeros((), jnp.bfloat16))
    partial_value = jnp.einsum(
        "kbj,kij->kbi", masked, dinv_leaf[0], preferred_element_type=jnp.float32
    )
    summed = lax.psum(partial_value, "col")
    row_slots = lax.axis_index("row") * width_row + lax.iota(jnp.int32, width_row)
    live_rows = (row_slots[None, None, :] < limit).astype(jnp.float32)
    solved = (summed * live_rows).astype(jnp.bfloat16)
    update = jnp.einsum("kbi,kri->kbr", solved, panel_leaf[0], preferred_element_type=jnp.float32)
    offset = lax.axis_index("col") * panel_rows
    targets = lax.dynamic_slice_in_dim(row_index[0], offset, panel_rows, 1)
    flat_update = jnp.transpose(update, (1, 0, 2)).reshape(columns, -1)
    accum = jnp.zeros((columns, sep_width), jnp.float32).at[:, targets.reshape(-1)].add(flat_update)
    piece = lax.psum_scatter(accum, "col", scatter_dimension=1, tiled=True)
    share = lax.psum(piece, ("leaf", "row"))
    reduced = (rhs_root.astype(jnp.float32) - share).astype(jnp.bfloat16)
    whole_reduced = lax.all_gather(reduced, "col", axis=1, tiled=True)
    y_root = jnp.dot(whole_reduced, dinv_root.T, preferred_element_type=jnp.float32).astype(
        jnp.bfloat16
    )
    return (solved[None], y_root)


def solution(mesh):
    in_specs = (
        P("leaf", None, None, "col"),
        P("leaf", None, "row", "col"),
        P("leaf", None, "col", "row"),
        P("leaf", None),
        P("leaf", None, None),
        P(None, "col"),
        P(("leaf", "row"), None),
    )
    out_specs = (P("leaf", None, None, "row"), P(None, ("leaf", "row")))
    return jax.shard_map(local, mesh=mesh, in_specs=in_specs, out_specs=out_specs, check_vma=False)
```

profile of v0, /device:TPU:0, one launch (start us, length us, event | category | flops | bytes accessed | tf_op | source)
XLA Modules:
  0.0 218.8 jit_solution(5079778243573968000)
XLA Ops:
  7.2 0.0 copy-start
  7.2 0.0 all-reduce.3.cloned.1.call-start
  7.2 0.9 compare_convert_fusion
  8.1 4.7 %fusion = f32[8,64,512]{2,1,0:T(8,128)} fusion(bf16[1,8,512,512]{3,2,1,0:T(8,128)(2,1)} %param.8, bf16[1,8,64,512]{3,2,1,0:T(8,128)(2,1)} %param.7, pred[8,512]{1,0:T(8,128)(4,1)S(1)} %get-tuple-element.3), kind=kOutput, calls=%fused_computation.1 | convolution fusion | flops 268697600 | bytes 5771264 | tf_op jit(solution)/shard_map/kbj,kij->kbi/dot_general | solution.py:16
  12.8 0.0 all-reduce.3.cloned.1.call-update
  12.8 0.0 reduce-scatter.2.cloned.1.call-start
  12.9 0.7 dynamic-slice_bitcast_fusion
  13.6 54.0 %all-reduce.3.cloned.1.call-done = f32[8,64,512]{2,1,0:T(8,128)} async-done(((f32[8,64,512]{2,1,0:T(8,128)}), f32[8,64,512]{2,1,0:T(8,128)}) %all-reduce.3.cloned.1.call-update) | async-done | bytes 1048592 | tf_op jit(solution)/shard_map/psum | solution.py:19
  67.6 0.0 copy-done
  67.6 2.0 fusion.4
  69.6 0.1 copy.13
  69.7 1.3 copy.12
  71.0 0.0 copy-start.2
  71.0 0.0 copy-start.1
  71.0 13.3 %scatter_custom_fusion = f32[64,4096]{0,1:T(8,128)} fusion(s32[2048]{0:T(1024)S(1)} %bitcast.29, f32[2048,64]{1,0:T(8,128)} %copy.12, f32[]{:T(128)} %constant.7.clone.1), kind=kCustom, calls=%fused_computation.7 | custom fusion | flops 131072 | bytes 1049088 | tf_op jit(solution)/shard_map/scatter-add | solution.py:27
  84.3 0.0 reduce-scatter.2.cloned.1.call-update
  84.3 0.0 all-reduce.5.cloned.1.call-start
  84.4 0.0 copy-done.2
  84.4 0.2 copy.10
  84.6 42.8 %reduce-scatter.2.cloned.1.call-done = f32[64,1024]{0,1:T(8,128)} async-done(((f32[64,4096]{0,1:T(8,128)}), f32[64,1024]{0,1:T(8,128)}) %reduce-scatter.2.cloned.1.call-update) | async-done | bytes 262160 | tf_op jit(solution)/shard_map/reduce_scatter | solution.py:28
  127.4 0.0 all-reduce.5.cloned.1.call-update
  127.4 0.0 copy-done.1
  127.4 0.9 fusion.11
  128.4 56.2 %all-reduce.5.cloned.1.call-done = f32[64,1024]{0,1:T(8,128)} async-done(((f32[64,1024]{0,1:T(8,128)}), f32[64,1024]{0,1:T(8,128)}) %all-reduce.5.cloned.1.call-update) | async-done | bytes 262160 | tf_op jit(solution)/shard_map/psum | solution.py:29
  184.5 1.1 subtract_convert_fusion
  185.6 22.4 %all_gather.3 = bf16[64,4096]{0,1:T(8,128)(2,1)S(1)} all-gather(bf16[64,1024]{0,1:T(8,128)(2,1)S(1)} %subtract_convert_fusion), channel_id=1, replica_groups=mesh['leaf'=2,'row'=4,'col'=4] {'col'}, dimensions={1}, use_global_device_ids=true | all-gather | bytes 655360 | tf_op jit(solution)/shard_map/all_gather | solution.py:31
  208.0 4.2 %convolution_convert_fusion = bf16[64,512]{1,0:T(8,128)(2,1)} fusion(bf16[64,4096]{0,1:T(8,128)(2,1)S(1)} %all_gather.3, bf16[512,4096]{1,0:T(8,128)(2,1)} %param.13), kind=kOutput, calls=%fused_computation.6 | convolution fusion | flops 268468224 | bytes 4784128 | tf_op jit(solution)/shard_map/dot_general | solution.py:32
  (3 shorter events, 0.0 us)
Async XLA Ops:
  7.2 60.5 %copy-start = (bf16[1,8,256,512]{3,2,1,0:T(8,128)(2,1)S(1)}, bf16[1,8,256,512]{3,2,1,0:T(8,128)(2,1)}, u32[]{:S(2)}) copy-start(bf16[1,8,256,512]{3,2,1,0:T(8,128)(2,1)} %param.9) | copy-start | bytes 6291460
  7.2 60.4 %all-reduce.3.cloned.1.call-start = ((), (), s32[]{:S(2)}) async-start(), calls=%async_computation.1 | async-start | bytes 2097152 | tf_op jit(solution)/shard_map/psum | solution.py:19
  12.8 114.6 %reduce-scatter.2.cloned.1.call-start = ((), (), s32[]{:S(2)}) async-start(), calls=%async_computation.2 | async-start | bytes 2621440 | tf_op jit(solution)/shard_map/reduce_scatter | solution.py:28
  71.0 13.4 %copy-start.2 = (bf16[64,1024]{1,0:T(8,128)(2,1)S(1)}, bf16[64,1024]{1,0:T(8,128)(2,1)}, u32[]{:S(2)}) copy-start(bf16[64,1024]{1,0:T(8,128)(2,1)} %param.12) | copy-start | bytes 393220
  71.0 56.5 %copy-start.1 = (f32[8,64,512]{2,1,0:T(8,128)S(1)}, f32[8,64,512]{2,1,0:T(8,128)}, u32[]{:S(2)}) copy-start(f32[8,64,512]{2,1,0:T(8,128)} %all-reduce.3.cloned.1.call-done) | copy-start | bytes 3145732
  84.3 100.2 %all-reduce.5.cloned.1.call-start = ((), (), s32[]{:S(2)}) async-start(), calls=%async_computation.3 | async-start | bytes 1048576 | tf_op jit(solution)/shard_map/psum | solution.py:29
Sparse Core Ops, SparseCore 0:
  13.0 54.6 all-reduce.2
  84.5 42.8 reduce-scatter.1
  130.5 53.9 all-reduce.4
where the time goes:
time: 219 us
  waiting for transfers between devices  153 us (70%)
  blocking collectives  22.4 us (10%)
  other arithmetic  16.2 us (7%)
  between operations  13.8 us (6%)
  matrix products  10.9 us (5%)
  local copies, waits for them, and re-layouts  2.27 us (1%)
    psum x1, waiting for transfers between devices, local(): share = lax.psum(piece, ('leaf', 'row'))  56.2 us
    psum x1, waiting for transfers between devices, local(): summed = lax.psum(partial_value, 'col')  54 us
    reduce_scatter x1, waiting for transfers between devices, local(): piece = lax.psum_scatter(accum, 'col', scatter_dimension=1, tiled=True)  42.8 us
    all_gather x1, blocking collectives, local(): whole_reduced = lax.all_gather(reduced, 'col', axis=1, tiled=True)  22.4 us
    scatter-add x1, other arithmetic, local(): jnp.zeros((columns, sep_width), jnp.float32).at[:, targets.reshape(-1)]  13.3 us
    dot_general x1, matrix products, local(): jnp.einsum('kbj,kij->kbi', masked, dinv_leaf[0], preferred_element_type=j...  4.71 us
  transfers between devices with their start and end apart: 3, of which 3 were waited for; matrix products, arithmetic and copies ran while one was open for 1% of the time, Pallas kernels for 0%

commit v1 on v0

--- a/solution.py
+++ b/solution.py
@@ -2,6 +2,21 @@
 import jax.numpy as jnp
 from jax import lax
 from jax.sharding import PartitionSpec as P
+
+
+def show_state(mat, row_axis):
+    ndev = lax.axis_size(row_axis)
+    found_now, piece_next = (mat, 0)
+    while 1 << piece_next < ndev:
+        all_blocks = []
+        dd = 0
+        while dd < ndev:
+            all_blocks.append((dd, dd ^ 1 << piece_next))
+            dd += 1
+        t1 = lax.ppermute(found_now, row_axis, all_blocks)
+        found_now = found_now + t1
+        piece_next = piece_next + 1
+    return found_now
 
 
 def local(rhs_leaf, dinv_leaf, panel_leaf, counts, row_index, rhs_root, dinv_root):
@@ -16,7 +31,7 @@
     partial_value = jnp.einsum(
         "kbj,kij->kbi", masked, dinv_leaf[0], preferred_element_type=jnp.float32
     )
-    summed = lax.psum(partial_value, "col")
+    summed = show_state(partial_value, "col")
     row_slots = lax.axis_index("row") * width_row + lax.iota(jnp.int32, width_row)
     live_rows = (row_slots[None, None, :] < limit).astype(jnp.float32)
     solved = (summed * live_rows).astype(jnp.bfloat16)

time: 219 us -> 240 us (1.096)
  waiting for transfers between devices: 153 us -> 169 us
  starting transfers between devices: 0.12 us -> 6.01 us
    ppermute x0 -> x2, waiting for transfers between devices: none -> 67.5 us  [show_state(): t1 = lax.ppermute(found_now, row_axis, all_blocks)]
    psum x1 -> x0, waiting for transfers between devices: 54 us -> none  [local(): summed = lax.psum(partial_value, 'col')]
    ppermute x0 -> x2, starting transfers between devices: none -> 5.93 us  [show_state(): t1 = lax.ppermute(found_now, row_axis, all_blocks)]
  transfers between devices with their start and end apart: 3 -> 4, of which waited for: 3 -> 4; matrix products, arithmetic and copies ran while one was open for 1% -> 0% of each run, Pallas kernels for 0% -> 0%
where the time goes in v1:
time: 240 us
  waiting for transfers between devices  169 us (70%)
  blocking collectives  22.4 us (9%)
  other arithmetic  16.9 us (7%)
  between operations  14.1 us (6%)
  matrix products  8.72 us (4%)
  starting transfers between devices  6.01 us (3%)
    ppermute x2, waiting for transfers between devices, show_state(): t1 = lax.ppermute(found_now, row_axis, all_blocks)  67.5 us
    psum x1, waiting for transfers between devices, local(): share = lax.psum(piece, ('leaf', 'row'))  56.9 us
    reduce_scatter x1, waiting for transfers between devices, local(): piece = lax.psum_scatter(accum, 'col', scatter_dimension=1, tiled=True)  44.7 us
    all_gather x1, blocking collectives, local(): whole_reduced = lax.all_gather(reduced, 'col', axis=1, tiled=True)  22.4 us
    scatter-add x1, other arithmetic, local(): jnp.zeros((columns, sep_width), jnp.float32).at[:, targets.reshape(-1)]  13.2 us
    ppermute x2, starting transfers between devices, show_state(): t1 = lax.ppermute(found_now, row_axis, all_blocks)  5.93 us
  transfers between devices with their start and end apart: 4, of which 4 were waited for; matrix products, arithmetic and copies ran while one was open for 0% of the time, Pallas kernels for 0%

profile of v1, /device:TPU:0, one launch (start us, length us, event | category | flops | bytes accessed | tf_op | source)
XLA Modules:
  0.0 239.6 jit_solution(15204526729501126434)
XLA Ops:
  7.2 0.0 copy-start
  7.2 0.0 reduce-scatter.2.cloned.1.call-start
  7.2 0.9 compare_convert_fusion
  8.1 3.7 %fusion = f32[8,64,512]{2,1,0:T(8,128)S(1)} fusion(bf16[1,8,512,512]{3,2,1,0:T(8,128)(2,1)} %param.8, bf16[1,8,64,512]{3,2,1,0:T(8,128)(2,1)} %param.7, pred[8,512]{1,0:T(8,128)(4,1)S(1)} %get-tuple-element.3), kind=kOutput, calls=%fused_computation.1 | convolution fusion | flops 268697600 | bytes 5771264 | tf_op jit(solution)/shard_map/kbj,kij->kbi/dot_general | solution.py:31
  11.8 3.1 %collective-permute-start = (f32[8,64,512]{2,1,0:T(8,128)S(1)}, f32[8,64,512]{2,1,0:T(8,128)S(1)}, u32[]{:S(2)}, u32[]{:S(2)}) collective-permute-start(f32[8,64,512]{2,1,0:T(8,128)S(1)} %fusion), channel_id=1, source_target_pairs={{0,1},{1,0},{2,3},{3,2},{4,5},{5,4},{6,7},{7,6},{8,9},{9,8},{10,11... | collective-permute-start | bytes 3145736 | tf_op jit(solution)/shard_map/ppermute | solution.py:16
  15.0 23.2 %collective-permute-done = f32[8,64,512]{2,1,0:T(8,128)S(1)} collective-permute-done((f32[8,64,512]{2,1,0:T(8,128)S(1)}, f32[8,64,512]{2,1,0:T(8,128)S(1)}, u32[]{:S(2)}, u32[]{:S(2)}) %collective-permute-start) | collective-permute-done | bytes 1048608 | tf_op jit(solution)/shard_map/ppermute | solution.py:16
  38.1 0.2 add.50
  38.3 2.8 %collective-permute-start.1 = (f32[8,64,512]{2,1,0:T(8,128)S(1)}, f32[8,64,512]{2,1,0:T(8,128)}, u32[]{:S(2)}, u32[]{:S(2)}) collective-permute-start(f32[8,64,512]{2,1,0:T(8,128)S(1)} %add.50), channel_id=1, source_target_pairs={{0,2},{1,3},{2,0},{3,1},{4,6},{5,7},{6,4},{7,5},{8,10},{9,11},{10,... | collective-permute-start | bytes 3145736 | tf_op jit(solution)/shard_map/ppermute | solution.py:16
  41.1 0.7 dynamic-slice_bitcast_fusion
  41.9 44.3 %collective-permute-done.1 = f32[8,64,512]{2,1,0:T(8,128)} collective-permute-done((f32[8,64,512]{2,1,0:T(8,128)S(1)}, f32[8,64,512]{2,1,0:T(8,128)}, u32[]{:S(2)}, u32[]{:S(2)}) %collective-permute-start.1) | collective-permute-done | bytes 1048608 | tf_op jit(solution)/shard_map/ppermute | solution.py:16
  86.2 1.5 multiply_convert_fusion
  87.7 0.0 copy-done
  87.7 0.0 copy-start.1
  87.7 0.8 fusion.4
  88.5 0.0 copy-done.1
  88.5 1.3 copy.12
  89.8 0.0 copy-start.2
  89.8 13.2 %scatter_custom_fusion = f32[64,4096]{0,1:T(8,128)} fusion(s32[2048]{0:T(1024)S(1)} %bitcast.30, f32[2048,64]{1,0:T(8,128)} %copy.12, f32[]{:T(128)} %constant.7.clone.1), kind=kCustom, calls=%fused_computation.7 | custom fusion | flops 131072 | bytes 1049088 | tf_op jit(solution)/shard_map/scatter-add | solution.py:42
  103.1 0.0 reduce-scatter.2.cloned.1.call-update
  103.1 0.0 all-reduce.2.cloned.1.call-start
  103.2 44.7 %reduce-scatter.2.cloned.1.call-done = f32[64,1024]{0,1:T(8,128)} async-done(((f32[64,4096]{0,1:T(8,128)}), f32[64,1024]{0,1:T(8,128)}) %reduce-scatter.2.cloned.1.call-update) | async-done | bytes 262160 | tf_op jit(solution)/shard_map/reduce_scatter | solution.py:43
  147.9 0.0 all-reduce.2.cloned.1.call-update
  147.9 0.0 copy-done.2
  147.9 0.2 copy.10
  148.1 56.9 %all-reduce.2.cloned.1.call-done = f32[64,1024]{0,1:T(8,128)} async-done(((f32[64,1024]{0,1:T(8,128)}), f32[64,1024]{0,1:T(8,128)}) %all-reduce.2.cloned.1.call-update) | async-done | bytes 262160 | tf_op jit(solution)/shard_map/psum | solution.py:44
  205.0 1.1 subtract_convert_fusion
  206.1 22.4 %all_gather.3 = bf16[64,4096]{0,1:T(8,128)(2,1)S(1)} all-gather(bf16[64,1024]{0,1:T(8,128)(2,1)S(1)} %subtract_convert_fusion), channel_id=1, replica_groups=mesh['leaf'=2,'row'=4,'col'=4] {'col'}, dimensions={1}, use_global_device_ids=true | all-gather | bytes 655360 | tf_op jit(solution)/shard_map/all_gather | solution.py:46
  228.5 4.2 %convolution_convert_fusion = bf16[64,512]{1,0:T(8,128)(2,1)} fusion(bf16[64,4096]{0,1:T(8,128)(2,1)S(1)} %all_gather.3, bf16[512,4096]{1,0:T(8,128)(2,1)} %param.13), kind=kOutput, calls=%fused_computation.6 | convolution fusion | flops 268468224 | bytes 4784128 | tf_op jit(solution)/shard_map/dot_general | solution.py:47
  (4 shorter events, 0.1 us)
Async XLA Ops:
  7.2 80.5 %copy-start = (bf16[1,8,256,512]{3,2,1,0:T(8,128)(2,1)S(1)}, bf16[1,8,256,512]{3,2,1,0:T(8,128)(2,1)}, u32[]{:S(2)}) copy-start(bf16[1,8,256,512]{3,2,1,0:T(8,128)(2,1)} %param.9) | copy-start | bytes 6291460
  7.2 140.7 %reduce-scatter.2.cloned.1.call-start = ((), (), s32[]{:S(2)}) async-start(), calls=%async_computation.1 | async-start | bytes 2621440 | tf_op jit(solution)/shard_map/reduce_scatter | solution.py:43
  11.8 26.3 %collective-permute-start = (f32[8,64,512]{2,1,0:T(8,128)S(1)}, f32[8,64,512]{2,1,0:T(8,128)S(1)}, u32[]{:S(2)}, u32[]{:S(2)}) collective-permute-start(f32[8,64,512]{2,1,0:T(8,128)S(1)} %fusion), channel_id=1, source_target_pairs={{0,1},{1,0},{2,3},{3,2},{4,5},{5,4},{6,7},{7,6},{8,9},{9,8},{10,11... | collective-permute-start | bytes 3145736 | tf_op jit(solution)/shard_map/ppermute | solution.py:16
  38.3 47.9 %collective-permute-start.1 = (f32[8,64,512]{2,1,0:T(8,128)S(1)}, f32[8,64,512]{2,1,0:T(8,128)}, u32[]{:S(2)}, u32[]{:S(2)}) collective-permute-start(f32[8,64,512]{2,1,0:T(8,128)S(1)} %add.50), channel_id=1, source_target_pairs={{0,2},{1,3},{2,0},{3,1},{4,6},{5,7},{6,4},{7,5},{8,10},{9,11},{10,... | collective-permute-start | bytes 3145736 | tf_op jit(solution)/shard_map/ppermute | solution.py:16
  87.7 0.8 copy-start.1
  89.8 58.1 %copy-start.2 = (bf16[64,1024]{1,0:T(8,128)(2,1)S(1)}, bf16[64,1024]{1,0:T(8,128)(2,1)}, u32[]{:S(2)}) copy-start(bf16[64,1024]{1,0:T(8,128)(2,1)} %param.12) | copy-start | bytes 393220
  103.1 101.9 %all-reduce.2.cloned.1.call-start = ((), (), s32[]{:S(2)}) async-start(), calls=%async_computation.2 | async-start | bytes 1048576 | tf_op jit(solution)/shard_map/psum | solution.py:44
Sparse Core Ops, SparseCore 0:
  103.2 44.6 reduce-scatter.1
  151.0 53.9 all-reduce.1
